TPU v7x, 32 devices: a whole 2x2x4 slice. The times are simulated.
32 devices in a mesh: fsdp: 4 (over y, x), ctx: 4 (over z), tp: 2 (over core).
Axes of the slice: x: 2, y: 2, z: 4, core: 2. Of those that a mesh axis runs over, the one named last changes fastest.
Arguments:
- tokens: bfloat16 [12288, 1536], P(('fsdp', 'ctx')), may hold values from -6 to 6
- routes: int32 [12288, 8], P(('fsdp', 'ctx')), may hold values from 0 to 39, all different within a row
- cotangent: bfloat16 [12288, 1536], P(('fsdp', 'ctx')), may hold values from -6 to 6
- attn_gain: bfloat16 [1536], P('fsdp'), may hold values from 0.5 to 1.5
- moe_gain: bfloat16 [1536], P('fsdp'), may hold values from 0.5 to 1.5
- w_query: bfloat16 [1536, 1536], P('fsdp', 'tp'), may hold values from -0.15625 to 0.15625
- w_key: bfloat16 [1536, 512], P('fsdp', 'tp'), may hold values from -0.15625 to 0.15625
- w_value: bfloat16 [1536, 512], P('fsdp', 'tp'), may hold values from -0.15625 to 0.15625
- w_out: bfloat16 [1536, 1536], P('tp', 'fsdp'), may hold values from -1.25 to 1.25
- w_router: bfloat16 [1536, 40], P('fsdp'), may hold values from -0.078125 to 0.078125
- w_gate: bfloat16 [40, 1536, 512], P('ctx', 'fsdp', 'tp'), may hold values from -0.15625 to 0.15625
- w_up: bfloat16 [40, 1536, 512], P('ctx', 'fsdp', 'tp'), may hold values from -0.15625 to 0.15625
- w_down: bfloat16 [40, 512, 1536], P('ctx', 'tp', 'fsdp'), may hold values from -1 to 1
Outputs:
- output: bfloat16 [12288, 1536], P(('fsdp', 'ctx'))
- grad_tokens: float32 [12288, 1536], P(('fsdp', 'ctx'))
- grad_attn_gain: float32 [1536], P(('fsdp', 'ctx'))
- grad_moe_gain: float32 [1536], P(('fsdp', 'ctx'))
- grad_query: float32 [1536, 1536], P(('fsdp', 'ctx'), 'tp')
- grad_key: float32 [1536, 512], P(('fsdp', 'ctx'), 'tp')
- grad_value: float32 [1536, 512], P(('fsdp', 'ctx'), 'tp')
- grad_out: float32 [1536, 1536], P('tp', ('fsdp', 'ctx'))
- grad_router: float32 [1536, 40], P(('fsdp', 'ctx'))
- grad_gate: float32 [40, 1536, 512], P('ctx', 'fsdp', 'tp')
- grad_up: float32 [40, 1536, 512], P('ctx', 'fsdp', 'tp')
- grad_down: float32 [40, 512, 1536], P('ctx', 'tp', 'fsdp')
Inputs may be any that keep to these rules, and one draw needn't show every extreme that they name: `routes`: each row names 8 different experts.
All inputs are finite; a program needn't handle non-finite values.
Results may differ from a plain program's by a relative error of at most 0.019.
Values may be sent and summed in bfloat16 or wider, within the bound.
A program may use at most 384 MiB of HBM per device.

v0:
```python
import jax
import jax.numpy as jnp
from jax import lax
from jax.sharding import PartitionSpec as P

H = 24
KV = 8
HD = 64
TOPK = 8
PROMPT = 2048
CONT_LEN = 512


norm_eps = 1e-06
rope_base = 10000.0


def rotation(position):
    halfway = HD // 2
    freq = rope_base ** (-jnp.arange(halfway, dtype=jnp.float32) * 2.0 / HD)
    angle = position.astype(jnp.float32)[:, None] * freq[None, :]
    return (jnp.cos(angle)[:, None, :], jnp.sin(angle)[:, None, :])


def rotate(values, cosine, sine):
    halfway = HD // 2
    former = values[..., :halfway]
    latter = values[..., halfway:]
    return jnp.concatenate(
        [former * cosine - latter * sine, latter * cosine + former * sine], axis=-1
    )


def over_rows(left, right):
    return lax.dot_general(
        left, right, (((0,), (0,)), ((), ())), preferred_element_type=jnp.float32
    )


def over_cols(left, right):
    return lax.dot_general(
        left, right, (((1,), (1,)), ((), ())), preferred_element_type=jnp.float32
    )


def on_device(
    tokens,
    routes,
    cotangent,
    attn_gain,
    moe_gain,
    w_query,
    w_key,
    w_value,
    w_out,
    w_router,
    w_gate,
    w_up,
    w_down,
):
    count, width = tokens.shape
    spread = lax.axis_size("ctx")
    place = lax.axis_index("ctx")
    tp_size = lax.axis_size("tp")
    group = count * spread
    (
        query_full,
        key_full,
        value_full,
        out_full,
        router_full,
        gate_full,
        up_full,
        down_full,
        attn_scale,
        moe_scale,
    ) = (
        lax.all_gather(w_query, "fsdp", axis=0, tiled=True),
        lax.all_gather(w_key, "fsdp", axis=0, tiled=True),
        lax.all_gather(w_value, "fsdp", axis=0, tiled=True),
        lax.all_gather(w_out, "fsdp", axis=1, tiled=True),
        lax.all_gather(w_router, "fsdp", axis=0, tiled=True),
        lax.all_gather(w_gate, "fsdp", axis=1, tiled=True),
        lax.all_gather(w_up, "fsdp", axis=1, tiled=True),
        lax.all_gather(w_down, "fsdp", axis=2, tiled=True),
        lax.all_gather(attn_gain, "fsdp", axis=0, tiled=True),
        lax.all_gather(moe_gain, "fsdp", axis=0, tiled=True),
    )
    index_all = jnp.arange(group, dtype=jnp.int32)
    segment_all = jnp.where(index_all < PROMPT, 0, 1 + (index_all - PROMPT) // CONT_LEN)
    position_all = jnp.where(
        index_all < PROMPT, index_all, PROMPT + (index_all - PROMPT) % CONT_LEN
    )
    first_row = place * count
    row_index = lax.dynamic_slice_in_dim(index_all, first_row, count)
    row_segment = lax.dynamic_slice_in_dim(segment_all, first_row, count)
    row_position = lax.dynamic_slice_in_dim(position_all, first_row, count)
    allowed = (index_all[None, :] <= row_index[:, None]) & (
        (segment_all[None, :] == 0) | (segment_all[None, :] == row_segment[:, None])
    )
    cosine, sine = rotation(row_position)
    scale = HD ** (-0.5)
    ratio = H // KV
    kv_local = key_full.shape[1] // HD
    token_f = tokens.astype(jnp.float32)
    inverse_one = lax.rsqrt(jnp.mean(token_f * token_f, axis=-1, keepdims=True) + norm_eps)
    unit_one = token_f * inverse_one
    normed_one = (unit_one * attn_scale.astype(jnp.float32)).astype(jnp.bfloat16)
    query_pre = jnp.dot(normed_one, query_full, preferred_element_type=jnp.float32).reshape(
        count, kv_local * ratio, HD
    )
    key_pre = jnp.dot(normed_one, key_full, preferred_element_type=jnp.float32).reshape(
        count, kv_local, HD
    )
    query_b = (
        rotate(query_pre, cosine, sine).astype(jnp.bfloat16).reshape(count, kv_local, ratio, HD)
    )
    key_b = rotate(key_pre, cosine, sine).astype(jnp.bfloat16).reshape(count, kv_local * HD)
    value_b = jnp.dot(normed_one, value_full, preferred_element_type=jnp.float32).astype(
        jnp.bfloat16
    )
    keys_all, values_all = (
        lax.all_gather(key_b, "ctx", axis=0, tiled=True),
        lax.all_gather(value_b, "ctx", axis=0, tiled=True),
    )
    query_heads = jnp.moveaxis(query_b, 1, 0)
    key_heads = jnp.moveaxis(keys_all.reshape(group, kv_local, HD), 1, 0)
    value_heads = jnp.moveaxis(values_all.reshape(group, kv_local, HD), 1, 0)

    def masked_scores(query_one, key_one):
        scores = (
            jnp.einsum("qrd,kd->qrk", query_one, key_one, preferred_element_type=jnp.float32)
            * scale
        )
        return jnp.where(allowed[:, None, :], scores, -1e30)

    def head_forward(operands):
        query_one, key_one, value_one = operands
        scores = masked_scores(query_one, key_one)
        highest = jnp.max(scores, axis=-1, keepdims=True)
        expo = jnp.exp(scores - highest)
        total = jnp.sum(expo, axis=-1, keepdims=True)
        probs = (expo / total).astype(jnp.bfloat16)
        mixed = jnp.einsum("qrk,kd->qrd", probs, value_one, preferred_element_type=jnp.float32)
        return (mixed, highest + jnp.log(total))

    head_out, log_sums = lax.map(head_forward, (query_heads, key_heads, value_heads))
    mixed_b = (
        jnp.moveaxis(head_out, 0, 1).reshape(count, kv_local * ratio * HD).astype(jnp.bfloat16)
    )
    attn_part = jnp.dot(mixed_b, out_full, preferred_element_type=jnp.float32)
    attn_total = lax.psum(attn_part, "tp")
    hidden = token_f + attn_total
    inverse_two = lax.rsqrt(jnp.mean(hidden * hidden, axis=-1, keepdims=True) + norm_eps)
    unit_two = hidden * inverse_two
    normed_two = (unit_two * moe_scale.astype(jnp.float32)).astype(jnp.bfloat16)
    logits = jnp.dot(normed_two, router_full, preferred_element_type=jnp.float32)
    experts = router_full.shape[1]
    expert_ids = jnp.arange(experts, dtype=jnp.int32)
    hits = routes[:, :, None] == expert_ids
    chosen = jnp.sum(jnp.where(hits, logits[:, None, :], 0.0), axis=-1)
    gates = jax.nn.softmax(chosen, axis=-1)
    gates_flat = gates.reshape(-1)
    capacity = max(tp_size, 9 * count * TOPK // (8 * experts) // tp_size * tp_size)
    local_experts = experts // spread
    picks = routes.reshape(-1)
    flags = (picks[:, None] == expert_ids).astype(jnp.int32)
    ranks = jnp.sum((jnp.cumsum(flags, axis=0) - 1) * flags, axis=1)
    kept = ranks < capacity
    slots = jnp.where(kept, picks * capacity + ranks, experts * capacity)
    sources = (
        jnp.full((experts * capacity,), -1, jnp.int32)
        .at[slots]
        .set(jnp.arange(picks.shape[0], dtype=jnp.int32), mode="drop")
    )
    filled = sources >= 0
    source_safe = jnp.maximum(sources, 0)
    owners = source_safe // TOPK
    outbound = jnp.where(filled[:, None], normed_two[owners], jnp.zeros((), jnp.bfloat16)).reshape(
        spread, local_experts, capacity, width
    )
    lower = jnp.zeros((), jnp.int32)
    inbound_sel = lax.all_to_all(outbound, "ctx", split_axis=0, concat_axis=0, tiled=True)
    gate_pre = jnp.einsum(
        "secd,edf->secf", inbound_sel, gate_full, preferred_element_type=jnp.float32
    )
    up_pre = jnp.einsum("secd,edf->secf", inbound_sel, up_full, preferred_element_type=jnp.float32)
    sigma = jax.nn.sigmoid(gate_pre)
    silu_gate = gate_pre * sigma
    active = (silu_gate * up_pre).astype(jnp.bfloat16)
    result_part = jnp.einsum(
        "secf,efd->secd", active, down_full, preferred_element_type=jnp.float32
    )
    slot_sum = lax.psum_scatter(result_part, "tp", scatter_dimension=2, tiled=True).astype(
        jnp.bfloat16
    )
    result_sel = lax.all_gather(slot_sum, "tp", axis=2, tiled=True)
    returned = lax.all_to_all(result_sel, "ctx", split_axis=0, concat_axis=0, tiled=True)
    returned_flat = returned.reshape(experts * capacity, width)
    mine = kept & (ranks >= lower) & (ranks < lower + capacity)
    slot_index = jnp.where(mine, picks * capacity + ranks, 0)
    picked = jnp.where(
        mine[:, None], returned_flat[slot_index], jnp.zeros((), jnp.bfloat16)
    ).reshape(count, TOPK, width)
    moe_part = jnp.sum(gates[:, :, None] * picked.astype(jnp.float32), axis=1)
    grad_output = cotangent.astype(jnp.float32)
    gate_grad_part = jnp.sum(picked.astype(jnp.float32) * grad_output[:, None, :], axis=-1)
    slot_weight = jnp.where(filled, gates_flat[source_safe], 0.0)
    grad_send = (
        (slot_weight[:, None] * grad_output[owners])
        .astype(jnp.bfloat16)
        .reshape(spread, local_experts, capacity, width)
    )
    grad_in_sel = lax.all_to_all(grad_send, "ctx", split_axis=0, concat_axis=0, tiled=True)
    active_grad = jnp.einsum(
        "secd,efd->secf", grad_in_sel, down_full, preferred_element_type=jnp.float32
    )
    up_grad = (active_grad * silu_gate).astype(jnp.bfloat16)
    gate_grad = (active_grad * up_pre * sigma * (1.0 + gate_pre * (1.0 - sigma))).astype(
        jnp.bfloat16
    )
    grad_down = jnp.einsum(
        "secf,secd->efd", active, grad_in_sel, preferred_element_type=jnp.float32
    )
    grad_gate = jnp.einsum(
        "secd,secf->edf", inbound_sel, gate_grad, preferred_element_type=jnp.float32
    )
    grad_up = jnp.einsum("secd,secf->edf", inbound_sel, up_grad, preferred_element_type=jnp.float32)
    input_part = jnp.einsum(
        "secf,edf->secd", gate_grad, gate_full, preferred_element_type=jnp.float32
    ) + jnp.einsum("secf,edf->secd", up_grad, up_full, preferred_element_type=jnp.float32)
    input_sum = lax.psum_scatter(input_part, "tp", scatter_dimension=2, tiled=True).astype(
        jnp.bfloat16
    )
    input_sel = lax.all_gather(input_sum, "tp", axis=2, tiled=True)
    grad_back = lax.all_to_all(input_sel, "ctx", split_axis=0, concat_axis=0, tiled=True)
    back_flat = grad_back.reshape(experts * capacity, width)
    back_picked = jnp.where(
        mine[:, None], back_flat[slot_index], jnp.zeros((), jnp.bfloat16)
    ).reshape(count, TOPK, width)
    normed_grad_part = jnp.sum(back_picked.astype(jnp.float32), axis=1)
    normed_grad = normed_grad_part
    output = (hidden + moe_part).astype(jnp.bfloat16)
    chosen_grad = gates * (gate_grad_part - jnp.sum(gates * gate_grad_part, axis=-1, keepdims=True))
    logit_grad = jnp.sum(jnp.where(hits, chosen_grad[:, :, None], 0.0), axis=1).astype(jnp.bfloat16)
    grad_router = over_rows(normed_two, logit_grad)
    normed_grad = normed_grad + over_cols(logit_grad, router_full)
    grad_moe_gain = jnp.sum(normed_grad * unit_two, axis=0)
    scaled_two = normed_grad * moe_scale.astype(jnp.float32)
    hidden_grad = grad_output + inverse_two * (
        scaled_two - unit_two * jnp.mean(scaled_two * unit_two, axis=-1, keepdims=True)
    )
    hidden_grad_b = hidden_grad.astype(jnp.bfloat16)
    grad_wout = over_rows(mixed_b, hidden_grad_b)
    mixed_grad = over_cols(hidden_grad_b, out_full).astype(jnp.bfloat16)
    mixed_heads = jnp.moveaxis(mixed_grad.reshape(count, kv_local, ratio, HD), 1, 0)

    def head_backward(operands):
        query_one, key_one, value_one, grad_one, log_sum = operands
        probs = jnp.exp(masked_scores(query_one, key_one) - log_sum)
        probs_b = probs.astype(jnp.bfloat16)
        prob_grad = jnp.einsum(
            "qrd,kd->qrk", grad_one, value_one, preferred_element_type=jnp.float32
        )
        value_grad = jnp.einsum(
            "qrk,qrd->kd", probs_b, grad_one, preferred_element_type=jnp.float32
        )
        delta = jnp.sum(probs * prob_grad, axis=-1, keepdims=True)
        score_grad = (probs * (prob_grad - delta) * scale).astype(jnp.bfloat16)
        query_grad = jnp.einsum(
            "qrk,kd->qrd", score_grad, key_one, preferred_element_type=jnp.float32
        )
        key_grad = jnp.einsum(
            "qrk,qrd->kd", score_grad, query_one, preferred_element_type=jnp.float32
        )
        return (query_grad, key_grad, value_grad)

    query_grads, key_grads, value_grads = lax.map(
        head_backward, (query_heads, key_heads, value_heads, mixed_heads, log_sums)
    )
    key_terms = jnp.moveaxis(key_grads, 0, 1).reshape(group, kv_local * HD)
    value_terms = jnp.moveaxis(value_grads, 0, 1).reshape(group, kv_local * HD)
    key_sum, value_sum = (
        lax.psum_scatter(
            key_terms.astype(jnp.bfloat16), "ctx", scatter_dimension=0, tiled=True
        ).astype(jnp.float32),
        lax.psum_scatter(
            value_terms.astype(jnp.bfloat16), "ctx", scatter_dimension=0, tiled=True
        ).astype(jnp.float32),
    )
    key_grad_b = (
        rotate(key_sum.reshape(count, kv_local, HD), cosine, -sine)
        .reshape(count, kv_local * HD)
        .astype(jnp.bfloat16)
    )
    value_grad_b = value_sum.astype(jnp.bfloat16)
    query_grad_b = (
        rotate(jnp.moveaxis(query_grads, 0, 1).reshape(count, kv_local * ratio, HD), cosine, -sine)
        .reshape(count, kv_local * ratio * HD)
        .astype(jnp.bfloat16)
    )
    grad_wquery = over_rows(normed_one, query_grad_b)
    grad_wkey = over_rows(normed_one, key_grad_b)
    grad_wvalue = over_rows(normed_one, value_grad_b)
    normed_one_part = (
        over_cols(query_grad_b, query_full)
        + over_cols(key_grad_b, key_full)
        + over_cols(value_grad_b, value_full)
    )
    normed_one_grad = lax.psum(normed_one_part.astype(jnp.bfloat16), "tp").astype(jnp.float32)
    grad_attn_gain = jnp.sum(normed_one_grad * unit_one, axis=0)
    scaled_one = normed_one_grad * attn_scale.astype(jnp.float32)
    token_grad = hidden_grad + inverse_one * (
        scaled_one - unit_one * jnp.mean(scaled_one * unit_one, axis=-1, keepdims=True)
    )
    owned = (
        lax.psum_scatter(grad_wquery, ("fsdp", "ctx"), scatter_dimension=0, tiled=True),
        lax.psum_scatter(grad_wkey, ("fsdp", "ctx"), scatter_dimension=0, tiled=True),
        lax.psum_scatter(grad_wvalue, ("fsdp", "ctx"), scatter_dimension=0, tiled=True),
        lax.psum_scatter(grad_wout, ("fsdp", "ctx"), scatter_dimension=1, tiled=True),
        lax.psum_scatter(grad_router, ("fsdp", "ctx"), scatter_dimension=0, tiled=True),
        lax.psum_scatter(grad_attn_gain, ("fsdp", "ctx"), scatter_dimension=0, tiled=True),
        lax.psum_scatter(grad_moe_gain, ("fsdp", "ctx"), scatter_dimension=0, tiled=True),
    )
    expert_owned = (
        lax.psum_scatter(
            grad_gate.astype(jnp.bfloat16), "fsdp", scatter_dimension=1, tiled=True
        ).astype(jnp.float32),
        lax.psum_scatter(
            grad_up.astype(jnp.bfloat16), "fsdp", scatter_dimension=1, tiled=True
        ).astype(jnp.float32),
        lax.psum_scatter(
            grad_down.astype(jnp.bfloat16), "fsdp", scatter_dimension=2, tiled=True
        ).astype(jnp.float32),
    )
    return (
        output,
        token_grad,
        owned[5],
        owned[6],
        owned[0],
        owned[1],
        owned[2],
        owned[3],
        owned[4],
        expert_owned[0],
        expert_owned[1],
        expert_owned[2],
    )


def solution(mesh):
    return jax.shard_map(
        on_device,
        mesh=mesh,
        in_specs=(
            P(("fsdp", "ctx"), None),
            P(("fsdp", "ctx"), None),
            P(("fsdp", "ctx"), None),
            P("fsdp"),
            P("fsdp"),
            P("fsdp", "tp"),
            P("fsdp", "tp"),
            P("fsdp", "tp"),
            P("tp", "fsdp"),
            P("fsdp", None),
            P("ctx", "fsdp", "tp"),
            P("ctx", "fsdp", "tp"),
            P("ctx", "tp", "fsdp"),
        ),
        out_specs=(
            P(("fsdp", "ctx"), None),
            P(("fsdp", "ctx"), None),
            P(("fsdp", "ctx")),
            P(("fsdp", "ctx")),
            P(("fsdp", "ctx"), "tp"),
            P(("fsdp", "ctx"), "tp"),
            P(("fsdp", "ctx"), "tp"),
            P("tp", ("fsdp", "ctx")),
            P(("fsdp", "ctx"), None),
            P("ctx", "fsdp", "tp"),
            P("ctx", "fsdp", "tp"),
            P("ctx", "tp", "fsdp"),
        ),
        check_vma=False,
    )
```

profile of v0, /device:TPU:0, one launch (start us, length us, event | category | flops | bytes accessed | tf_op | source)
XLA Modules:
  0.0 4612.6 jit_solution(14763143128388135735)
XLA Ops:
  76.3 35.5 all-gather.12.cloned.1.call-done
  116.1 34.8 all-gather.14.cloned.1.call-done
  150.9 175.2 %while.30 = (s32[]{:T(128)}, bf16[4,768,3,64]{1,3,2,0:T(8,128)(2,1)S(1)}, f32[4,768,3,1]{1,2,3,0:T(4,128)}, bf16[4,768,3,64]{1,3,2,0:T(8,128)(2,1)S(1)}, bf16[4,...) while((s32[]{:T(128)}, ...), condition=%wide.region_4.5_spmd.clone.clone, body=%wide.region_1.4_spmd.clone.sunk.clone | while | flops 1906308864 | bytes 96149608 | solution.py:147
  347.3 20.9 reduce-window.6
  370.8 23.0 scatter_custom_fusion
  409.4 35.9 gather_fusion.2
  446.1 23.6 gather_fusion
  469.7 22.9 gather.24
  521.7 43.3 gather_fusion.3
  565.0 34.9 gather.29
  600.1 23.7 multiply_convert_fusion.1
  623.8 356.9 %all-to-all-done = bf16[4,10,172,1536]{3,2,1,0:T(8,128)(2,1)} async-done(((bf16[4,10,172,1536]{3,2,1,0:T(8,128)(2,1)}), bf16[4,10,172,1536]{3,2,1,0:T(8,128)(2,1)}, u32[]{:S(2)}, u32[]{:S(2)}) %all-to-all-start) | async-done | bytes 21135392 | tf_op jit(solution)/shard_map/all_to_all | solution.py:183
  1007.8 66.7 %all-gather.24.cloned.1.call-done = bf16[10,256,1536]{2,1,0:T(8,128)(2,1)} async-done(((bf16[10,256,384]{2,1,0:T(8,128)(2,1)}), bf16[10,256,1536]{2,1,0:T(8,128)(2,1)}) %all-gather.24.cloned.1.call-update) | async-done | bytes 7864336 | tf_op jit(solution)/shard_map/all_gather | solution.py:85
  1074.5 380.3 %all-to-all-done.2 = bf16[4,10,172,1536]{3,2,1,0:T(8,128)(2,1)} async-done(((bf16[4,10,172,1536]{3,2,1,0:T(8,128)(2,1)}), bf16[4,10,172,1536]{3,2,1,0:T(8,128)(2,1)}, u32[]{:S(2)}, u32[]{:S(2)}) %all-to-all-start.2) | async-done | bytes 21135392 | tf_op jit(solution)/shard_map/all_to_all | solution.py:214
  1488.3 21.2 fusion.114
  1509.5 31.8 add_bitcast_fusion
  1541.3 47.5 %copy.67 = f32[4,10,172,1536]{3,0,1,2:T(4,128)} copy(f32[4,10,172,1536]{3,2,0,1:T(8,128)} %add_bitcast_fusion) | data formatting | bytes 84541440 | tf_op jit(solution)/shard_map/add | solution.py:229
  1609.4 47.2 %copy.63 = f32[4,10,172,1536]{3,0,1,2:T(4,128)} copy(f32[4,10,172,1536]{3,2,0,1:T(8,128)} %convolution_bitcast_fusion) | data formatting | bytes 84541440 | tf_op jit(solution)/shard_map/secf,efd->secd/transpose | solution.py:191
  1656.6 217.5 %all-reduce.13 = (bf16[4,10,172,1536]{3,0,1,2:T(4,128)(2,1)}, bf16[4,10,172,1536]{3,0,1,2:T(4,128)(2,1)}) all-reduce(f32[4,10,172,1536]{3,0,1,2:T(4,128)} %copy.67, f32[4,10,172,1536]{3,0,1,2:T(4,128)} %copy.63), channel_id=3, replica_groups=mesh['fsdp'=4,'ctx'=4,'tp'=2] {'tp'}, use_global_device_ids=true, to_apply=%region_16.17.clone | all-reduce | flops 21135360 | bytes 126812160
  1883.8 34.1 all-gather.28.cloned.1.call-done
  1956.5 37.5 all-gather.26.cloned.1.call-done
  1994.1 20.8 copy.64
  2014.9 399.2 %all-to-all-done.3 = bf16[4,10,172,1536]{3,2,1,0:T(8,128)(2,1)} async-done(((bf16[4,10,172,1536]{3,2,1,0:T(8,128)(2,1)}), bf16[4,10,172,1536]{3,2,1,0:T(8,128)(2,1)}, u32[]{:S(2)}, u32[]{:S(2)}) %all-to-all-start.3) | async-done | bytes 21135392 | tf_op jit(solution)/shard_map/all_to_all | solution.py:236
  2422.8 23.0 reshape.458
  2445.9 47.0 %gather_fusion.4 = bf16[6144,1536]{1,0:T(8,128)(2,1)} fusion(bf16[6880,1536]{1,0:T(8,128)(2,1)} %reshape.458, s32[6144]{0:T(1024)S(1)} %broadcast_clamp_fusion), kind=kCustom, calls=%fused_computation.4 | custom fusion | bytes 37773312 | tf_op jit(solution)/shard_map/gather | solution.py:239
  2492.9 395.6 %all-to-all-done.1 = bf16[4,10,172,1536]{3,2,1,0:T(8,128)(2,1)} async-done(((bf16[4,10,172,1536]{3,2,1,0:T(8,128)(2,1)}), bf16[4,10,172,1536]{3,2,1,0:T(8,128)(2,1)}, u32[]{:S(2)}, u32[]{:S(2)}) %all-to-all-start.1) | async-done | bytes 21135392 | tf_op jit(solution)/shard_map/all_to_all | solution.py:198
  2888.5 23.0 reshape.457
  2911.5 47.1 %gather_fusion.1 = bf16[6144,1536]{1,0:T(8,128)(2,1)} fusion(bf16[6880,1536]{1,0:T(8,128)(2,1)} %reshape.457, s32[6144]{0:T(1024)S(1)} %broadcast_clamp_fusion), kind=kCustom, calls=%fused_computation.1 | custom fusion | bytes 37773312 | tf_op jit(solution)/shard_map/gather | solution.py:203
  2958.6 38.7 convert_reduce_fusion
  3021.5 554.4 %while.31 = (s32[]{:T(128)}, f32[4,768,3,64]{1,3,2,0:T(8,128)}, bf16[4,3072,64]{1,2,0:T(8,128)(2,1)}, bf16[4,3072,64]{1,2,0:T(8,128)(2,1)}, bf16[4,768,3,64]{1,3...) while((s32[]{:T(128)}, f32[4,768,3,64]{1,3,2,0:T(8,128)}, ...), condition=%wide.region_24.25_spmd.clone.clone, body=%wide.region_22.24_spmd.clone.sunk.clone | while | flops 4723321344 | bytes 334966944 | solution.py:278
  3064.9 48.0 %fusion.275 = bf16[4,3072,64]{1,2,0:T(8,128)(2,1)} fusion(bf16[4,3072,64]{1,2,0:T(8,128)(2,1)} %get-tuple-element.497, s32[]{:T(128)S(6)} %copy.122, f32[768,3,3072]{2,0,1:T(8,128)} %fusion.271, f32[768,3,3072]{2,0,1:T(8,128)} %fusion.272, f32[768,3]{0,1:T(4,128)} %copy-done.44, pred[768,3072]{1,0:T(8,128)(4,1)S(1)} %fusion.273, ...), kind=kOutput, calls=%fused_computation.53.clone.1.clone | convolution fusion | flops 983831808 | bytes 119071744 | tf_op jit(solution)/shard_map/while/body/eval_jaxpr/qrk,qrd->kd/dot_general | solution.py:273
  3112.9 47.4 %fusion.274 = f32[4,768,3,64]{1,3,2,0:T(8,128)} fusion(f32[4,768,3,64]{1,3,2,0:T(8,128)} %get-tuple-element.496, s32[]{:T(128)S(6)} %copy.122, f32[768,3,3072]{2,0,1:T(8,128)} %fusion.271, f32[768,3,3072]{2,0,1:T(8,128)} %fusion.272, f32[768,3]{0,1:T(4,128)} %copy-done.44, pred[768,3072]{1,0:T(8,128)(4,1)S(1)} %fusion.273, ...), kind=kOutput, calls=%fused_computation.55.clone.1.clone | convolution fusion | flops 983831808 | bytes 118973440 | tf_op jit(solution)/shard_map/while/body/eval_jaxpr/qrk,kd->qrd/dot_general | solution.py:270
  3203.3 48.0 %fusion.275 = bf16[4,3072,64]{1,2,0:T(8,128)(2,1)} fusion(bf16[4,3072,64]{1,2,0:T(8,128)(2,1)} %get-tuple-element.497, s32[]{:T(128)S(6)} %copy.122, f32[768,3,3072]{2,0,1:T(8,128)} %fusion.271, f32[768,3,3072]{2,0,1:T(8,128)} %fusion.272, f32[768,3]{0,1:T(4,128)} %copy-done.44, pred[768,3072]{1,0:T(8,128)(4,1)S(1)} %fusion.273, ...), kind=kOutput, calls=%fused_computation.53.clone.1.clone | convolution fusion | flops 983831808 | bytes 119071744 | tf_op jit(solution)/shard_map/while/body/eval_jaxpr/qrk,qrd->kd/dot_general | solution.py:273
  3251.4 47.4 %fusion.274 = f32[4,768,3,64]{1,3,2,0:T(8,128)} fusion(f32[4,768,3,64]{1,3,2,0:T(8,128)} %get-tuple-element.496, s32[]{:T(128)S(6)} %copy.122, f32[768,3,3072]{2,0,1:T(8,128)} %fusion.271, f32[768,3,3072]{2,0,1:T(8,128)} %fusion.272, f32[768,3]{0,1:T(4,128)} %copy-done.44, pred[768,3072]{1,0:T(8,128)(4,1)S(1)} %fusion.273, ...), kind=kOutput, calls=%fused_computation.55.clone.1.clone | convolution fusion | flops 983831808 | bytes 118973440 | tf_op jit(solution)/shard_map/while/body/eval_jaxpr/qrk,kd->qrd/dot_general | solution.py:270
  3341.8 48.0 %fusion.275 = bf16[4,3072,64]{1,2,0:T(8,128)(2,1)} fusion(bf16[4,3072,64]{1,2,0:T(8,128)(2,1)} %get-tuple-element.497, s32[]{:T(128)S(6)} %copy.122, f32[768,3,3072]{2,0,1:T(8,128)} %fusion.271, f32[768,3,3072]{2,0,1:T(8,128)} %fusion.272, f32[768,3]{0,1:T(4,128)} %copy-done.44, pred[768,3072]{1,0:T(8,128)(4,1)S(1)} %fusion.273, ...), kind=kOutput, calls=%fused_computation.53.clone.1.clone | convolution fusion | flops 983831808 | bytes 119071744 | tf_op jit(solution)/shard_map/while/body/eval_jaxpr/qrk,qrd->kd/dot_general | solution.py:273
  3389.8 47.4 %fusion.274 = f32[4,768,3,64]{1,3,2,0:T(8,128)} fusion(f32[4,768,3,64]{1,3,2,0:T(8,128)} %get-tuple-element.496, s32[]{:T(128)S(6)} %copy.122, f32[768,3,3072]{2,0,1:T(8,128)} %fusion.271, f32[768,3,3072]{2,0,1:T(8,128)} %fusion.272, f32[768,3]{0,1:T(4,128)} %copy-done.44, pred[768,3072]{1,0:T(8,128)(4,1)S(1)} %fusion.273, ...), kind=kOutput, calls=%fused_computation.55.clone.1.clone | convolution fusion | flops 983831808 | bytes 118973440 | tf_op jit(solution)/shard_map/while/body/eval_jaxpr/qrk,kd->qrd/dot_general | solution.py:270
  3480.2 48.0 %fusion.275 = bf16[4,3072,64]{1,2,0:T(8,128)(2,1)} fusion(bf16[4,3072,64]{1,2,0:T(8,128)(2,1)} %get-tuple-element.497, s32[]{:T(128)S(6)} %copy.122, f32[768,3,3072]{2,0,1:T(8,128)} %fusion.271, f32[768,3,3072]{2,0,1:T(8,128)} %fusion.272, f32[768,3]{0,1:T(4,128)} %copy-done.44, pred[768,3072]{1,0:T(8,128)(4,1)S(1)} %fusion.273, ...), kind=kOutput, calls=%fused_computation.53.clone.1.clone | convolution fusion | flops 983831808 | bytes 119071744 | tf_op jit(solution)/shard_map/while/body/eval_jaxpr/qrk,qrd->kd/dot_general | solution.py:273
  3528.2 47.5 %fusion.274 = f32[4,768,3,64]{1,3,2,0:T(8,128)} fusion(f32[4,768,3,64]{1,3,2,0:T(8,128)} %get-tuple-element.496, s32[]{:T(128)S(6)} %copy.122, f32[768,3,3072]{2,0,1:T(8,128)} %fusion.271, f32[768,3,3072]{2,0,1:T(8,128)} %fusion.272, f32[768,3]{0,1:T(4,128)} %copy-done.44, pred[768,3072]{1,0:T(8,128)(4,1)S(1)} %fusion.273, ...), kind=kOutput, calls=%fused_computation.55.clone.1.clone | convolution fusion | flops 983831808 | bytes 118973440 | tf_op jit(solution)/shard_map/while/body/eval_jaxpr/qrk,kd->qrd/dot_general | solution.py:270
  3694.0 38.2 reduce-scatter.33.cloned.1.call-done
  3746.0 72.2 %reduce-scatter.27.cloned.1.call-done = bf16[10,384,256]{2,1,0:T(8,128)(2,1)} async-done(((bf16[10,1536,256]{2,1,0:T(8,128)(2,1)}), bf16[10,384,256]{2,1,0:T(8,128)(2,1)}) %reduce-scatter.27.cloned.1.call-update) | async-done | bytes 1966096 | tf_op jit(solution)/shard_map/reduce_scatter | solution.py:326
  3822.0 82.1 %reduce-scatter.29.cloned.1.call-done = bf16[10,384,256]{2,1,0:T(8,128)(2,1)} async-done(((bf16[10,1536,256]{2,1,0:T(8,128)(2,1)}), bf16[10,384,256]{2,1,0:T(8,128)(2,1)}) %reduce-scatter.29.cloned.1.call-update) | async-done | bytes 1966096 | tf_op jit(solution)/shard_map/reduce_scatter | solution.py:329
  3908.0 124.6 %reduce-scatter.31.cloned.1.call-done = f32[96,40]{1,0:T(8,128)} async-done(((f32[1536,40]{1,0:T(8,128)}), f32[96,40]{1,0:T(8,128)}) %reduce-scatter.31.cloned.1.call-update) | async-done | bytes 15376
  4034.1 21.6 all-reduce.12.cloned.1.call-done
  4058.9 77.8 %all-reduce.4 = (f32[1536]{0:T(1024)S(1)}, f32[1536]{0:T(1024)S(1)}) all-reduce(f32[1536]{0:T(1024)S(1)} %get-tuple-element.169, f32[1536]{0:T(1024)S(1)} %copy-done.62), channel_id=6, replica_groups=mesh['fsdp'=4,'ctx'=4,'tp'=2] {'fsdp','ctx'}, use_global_device_ids=true, to_apply=%region_30.31.clone | all-reduce | flops 3072 | bytes 24576
  4144.4 43.9 reduce-scatter.21.cloned.1.call-done
  4188.3 130.3 %reduce-scatter.23.cloned.1.call-done = f32[96,256]{1,0:T(8,128)} async-done(((f32[1536,256]{1,0:T(8,128)}), f32[96,256]{1,0:T(8,128)}) %reduce-scatter.23.cloned.1.call-update) | async-done | bytes 98320 | tf_op jit(solution)/shard_map/reduce_scatter | solution.py:319
  4318.6 143.4 %reduce-scatter.19.cloned.1.call-done = f32[96,768]{1,0:T(8,128)} async-done(((f32[1536,768]{1,0:T(8,128)}), f32[96,768]{1,0:T(8,128)}) %reduce-scatter.19.cloned.1.call-update) | async-done | bytes 294928 | tf_op jit(solution)/shard_map/reduce_scatter | solution.py:317
  4462.0 143.5 %reduce-scatter.25.cloned.1.call-done = f32[768,96]{0,1:T(8,128)} async-done(((f32[768,1536]{0,1:T(8,128)}), f32[768,96]{0,1:T(8,128)}) %reduce-scatter.25.cloned.1.call-update) | async-done | bytes 294928 | tf_op jit(solution)/shard_map/reduce_scatter | solution.py:320
  (362 shorter events, 801.9 us)
Async XLA Ops:
  7.2 66.5 %all-gather.16.cloned.1.call-start = ((), (), s32[]{:S(2)}) async-start(), calls=%async_computation.16 | async-start | bytes 1966080 | tf_op jit(solution)/shard_map/all_gather | solution.py:124
  10.1 38.6 copy-start.60
  19.7 29.0 copy-start.54
  32.8 15.9 copy-start.4
  36.2 75.5 %all-gather.12.cloned.1.call-start = ((), (), s32[]{:S(2)}) async-start(), calls=%async_computation.14 | async-start | bytes 2949120 | tf_op jit(solution)/shard_map/all_gather | solution.py:78
  37.0 114.0 %all-gather.14.cloned.1.call-start = ((), (), s32[]{:S(2)}) async-start(), calls=%async_computation.15 | async-start | bytes 1966080 | tf_op jit(solution)/shard_map/all_gather | solution.py:123
  50.7 275.5 %all-gather.18.cloned.1.call-start = ((), (), s32[]{:S(2)}) async-start(), calls=%async_computation.17 | async-start | bytes 2949120 | tf_op jit(solution)/shard_map/all_gather | solution.py:81
  51.3 351.2 %all-reduce.10.cloned.1.call-start = ((), (), s32[]{:S(2)}) async-start(), calls=%async_computation.18 | async-start | bytes 9437184 | tf_op jit(solution)/shard_map/psum | solution.py:152
  333.9 60.0 %copy-start.63 = (bf16[384,40]{0,1:T(8,128)(2,1)S(1)}, bf16[384,40]{0,1:T(8,128)(2,1)}, u32[]{:S(2)}) copy-start(bf16[384,40]{0,1:T(8,128)(2,1)} %param.26) | copy-start | bytes 92164
  333.9 68.6 %copy-start.5 = (bf16[768,1536]{1,0:T(8,128)(2,1)S(1)}, bf16[768,1536]{1,0:T(8,128)(2,1)}, u32[]{:S(2)}) copy-start(bf16[768,1536]{1,0:T(8,128)(2,1)} %param.17) | copy-start | bytes 7077892
  345.1 60.4 %copy-start.48 = (f32[1536]{0:T(1024)}, f32[1536]{0:T(1024)S(1)}, u32[]{:S(2)}) copy-start(f32[1536]{0:T(1024)S(1)} %reshape.521) | copy-start | bytes 18436
  406.0 40.1 copy-start
  409.2 36.1 copy-start.15
  510.4 470.3 %all-to-all-start = ((bf16[4,10,172,1536]{3,2,1,0:T(8,128)(2,1)}), bf16[4,10,172,1536]{3,2,1,0:T(8,128)(2,1)}, u32[]{:S(2)}, u32[]{:S(2)}) async-start(bf16[4,10,172,1536]{3,2,1,0:T(8,128)(2,1)} %broadcast_select_fusion), calls=%async_computation | async-start | bytes 43253760 | tf_op jit(solution)/shard_map/all_to_all | solution.py:183
  518.3 472.9 %all-gather.20.cloned.1.call-start = ((), (), s32[]{:S(2)}) async-start(), calls=%async_computation.19 | async-start | bytes 9830400 | tf_op jit(solution)/shard_map/all_gather | solution.py:83
  565.0 34.9 copy-start.50
  623.8 366.2 %copy-start.65 = (u32[32]{0:T(128)S(1)}, u32[32]{0:T(128)}, u32[]{:S(2)}) copy-start(u32[32]{0:T(128)} %constant.152) | copy-start | bytes 388
  980.7 474.1 %all-to-all-start.2 = ((bf16[4,10,172,1536]{3,2,1,0:T(8,128)(2,1)}), bf16[4,10,172,1536]{3,2,1,0:T(8,128)(2,1)}, u32[]{:S(2)}, u32[]{:S(2)}) async-start(bf16[4,10,172,1536]{3,2,1,0:T(8,128)(2,1)} %multiply_convert_fusion.1), calls=%async_computation.2 | async-start | bytes 43253760 | tf_op jit(solution)/shard_map/all_to_all | solution.py:214
  988.4 86.1 %all-gather.24.cloned.1.call-start = ((), (), s32[]{:S(2)}) async-start(), calls=%async_computation.21 | async-start | bytes 9830400 | tf_op jit(solution)/shard_map/all_gather | solution.py:85
  989.2 480.2 %all-gather.22.cloned.1.call-start = ((), (), s32[]{:S(2)}) async-start(), calls=%async_computation.20 | async-start | bytes 9830400 | tf_op jit(solution)/shard_map/all_gather | solution.py:84
  989.9 928.0 %all-gather.28.cloned.1.call-start = ((), (), s32[]{:S(2)}) async-start(), calls=%async_computation.23 | async-start | bytes 31703040 | tf_op jit(solution)/shard_map/all_gather | solution.py:235
  1488.3 21.2 copy-start.12
  1938.7 475.4 %all-to-all-start.3 = ((bf16[4,10,172,1536]{3,2,1,0:T(8,128)(2,1)}), bf16[4,10,172,1536]{3,2,1,0:T(8,128)(2,1)}, u32[]{:S(2)}, u32[]{:S(2)}) async-start(bf16[4,10,172,1536]{3,2,1,0:T(8,128)(2,1)} %copy.68), calls=%async_computation.3 | async-start | bytes 43253760 | tf_op jit(solution)/shard_map/all_to_all | solution.py:236
  1946.5 47.6 %all-gather.26.cloned.1.call-start = ((), (), s32[]{:S(2)}) async-start(), calls=%async_computation.22 | async-start | bytes 31703040 | tf_op jit(solution)/shard_map/all_gather | solution.py:197
  2014.9 407.1 %copy-start.46 = (s32[6144]{0:T(1024)S(1)}, s32[6144]{0:T(1024)}, u32[]{:S(2)}) copy-start(s32[6144]{0:T(1024)} %copy-done.45) | copy-start | bytes 73732
  2014.9 407.9 %copy-start.53 = (s32[6144,1]{0,1:T(1,128)S(1)}, s32[6144,1]{0,1:T(1,128)}, u32[]{:S(2)}) copy-start(s32[6144,1]{0,1:T(1,128)} %get-tuple-element.242) | copy-start | bytes 73732
  2414.0 474.5 %all-to-all-start.1 = ((bf16[4,10,172,1536]{3,2,1,0:T(8,128)(2,1)}), bf16[4,10,172,1536]{3,2,1,0:T(8,128)(2,1)}, u32[]{:S(2)}, u32[]{:S(2)}) async-start(bf16[4,10,172,1536]{3,2,1,0:T(8,128)(2,1)} %copy.64), calls=%async_computation.1 | async-start | bytes 43253760 | tf_op jit(solution)/shard_map/all_to_all | solution.py:198
  2421.9 1241.2 %reduce-scatter.15.cloned.1.call-start = ((), (), s32[]{:S(2)}) async-start(), calls=%async_computation.24 | async-start | bytes 1966080 | tf_op jit(solution)/shard_map/reduce_scatter | solution.py:284
  2911.5 47.1 %copy-start.16 = (f32[768,8]{1,0:T(8,128)S(1)}, f32[768,8]{1,0:T(8,128)}, u32[]{:S(2)}) copy-start(f32[768,8]{1,0:T(8,128)} %copy-done.15) | copy-start | bytes 73732
  2958.6 38.7 copy-start.2
  3022.6 16.6 copy-start.44
  3026.8 12.4 copy-start.25
  3161.0 16.6 copy-start.44
  3165.3 12.4 copy-start.25
  3299.5 16.6 copy-start.44
  3303.7 12.4 copy-start.25
  3437.9 16.6 copy-start.44
  3575.9 91.3 %reduce-scatter.17.cloned.1.call-start = ((), (), s32[]{:S(2)}) async-start(), calls=%async_computation.25 | async-start | bytes 1966080 | tf_op jit(solution)/shard_map/reduce_scatter | solution.py:287
  3576.5 155.7 %reduce-scatter.33.cloned.1.call-start = ((), (), s32[]{:S(2)}) async-start(), calls=%async_computation.34 | async-start | bytes 9830400
  3619.4 198.8 %reduce-scatter.27.cloned.1.call-start = ((), (), s32[]{:S(2)}) async-start(), calls=%async_computation.31 | async-start | bytes 9830400 | tf_op jit(solution)/shard_map/reduce_scatter | solution.py:326
  3635.2 269.0 %reduce-scatter.29.cloned.1.call-start = ((), (), s32[]{:S(2)}) async-start(), calls=%async_computation.32 | async-start | bytes 9830400 | tf_op jit(solution)/shard_map/reduce_scatter | solution.py:329
  3650.8 381.8 %reduce-scatter.31.cloned.1.call-start = ((), (), s32[]{:S(2)}) async-start(), calls=%async_computation.33 | async-start | bytes 835584
  3654.2 401.5 %all-reduce.12.cloned.1.call-start = ((), (), s32[]{:S(2)}) async-start(), calls=%async_computation.26 | async-start | bytes 4718592 | tf_op jit(solution)/shard_map/psum | solution.py:310
  3673.9 514.4 %reduce-scatter.21.cloned.1.call-start = ((), (), s32[]{:S(2)}) async-start(), calls=%async_computation.28 | async-start | bytes 1671168 | tf_op jit(solution)/shard_map/reduce_scatter | solution.py:318
  3676.2 642.4 %reduce-scatter.23.cloned.1.call-start = ((), (), s32[]{:S(2)}) async-start(), calls=%async_computation.29 | async-start | bytes 1671168 | tf_op jit(solution)/shard_map/reduce_scatter | solution.py:319
  3679.7 782.3 %reduce-scatter.19.cloned.1.call-start = ((), (), s32[]{:S(2)}) async-start(), calls=%async_computation.27 | async-start | bytes 5013504 | tf_op jit(solution)/shard_map/reduce_scatter | solution.py:317
  3684.3 921.2 %reduce-scatter.25.cloned.1.call-start = ((), (), s32[]{:S(2)}) async-start(), calls=%async_computation.30 | async-start | bytes 5013504 | tf_op jit(solution)/shard_map/reduce_scatter | solution.py:320
  3822.0 236.8 %copy-start.62 = (f32[1536]{0:T(1024)S(1)}, f32[1536]{0:T(1024)}, u32[]{:S(2)}) copy-start(f32[1536]{0:T(1024)} %get-tuple-element.167) | copy-start | bytes 18436
  (51 other events, 250.2 us)
Sparse Core Ops, SparseCore 0:
  36.3 37.2 all-gather.15
  75.5 36.1 all-gather.11
  113.9 37.0 all-gather.13
  152.6 36.0 all-gather.17
  333.0 28.0 all-reduce.9
  520.7 83.5 all-gather.19
  991.1 83.3 all-gather.23
  1076.3 83.1 all-gather.21
  1883.9 33.9 all-gather.27
  1956.7 37.3 all-gather.25
  3576.0 34.7 reduce-scatter.14
  3612.9 34.2 reduce-scatter.16
  3650.3 81.9 reduce-scatter.32
  3735.1 83.0 reduce-scatter.26
  3821.0 83.0 reduce-scatter.28
  3908.7 123.8 reduce-scatter.30
  4034.8 20.8 all-reduce.11
  4060.9 127.3 reduce-scatter.20
  4193.7 124.9 reduce-scatter.22
  4324.2 137.7 reduce-scatter.18
  4467.7 137.6 reduce-scatter.24
where the time goes:
time: 4620 us; the launch traced here: 4610 us
  waiting for transfers between devices  2560 us (55%)
  matrix products  867 us (19%)
  local copies, waits for them, and re-layouts  543 us (12%)
  blocking collectives  344 us (7%)
  other arithmetic  244 us (5%)
    all_to_all x1, waiting for transfers between devices, on_device(): lax.all_to_all(input_sel, 'ctx', split_axis=0, concat_axis=0, tiled=True)  399 us
    all_to_all x1, waiting for transfers between devices, on_device(): lax.all_to_all(result_sel, 'ctx', split_axis=0, concat_axis=0, tiled=True)  396 us
    all_to_all x1, waiting for transfers between devices, on_device(): lax.all_to_all(grad_send, 'ctx', split_axis=0, concat_axis=0, tiled=True)  380 us
    all_to_all x1, waiting for transfers between devices, on_device(): lax.all_to_all(outbound, 'ctx', split_axis=0, concat_axis=0, tiled=True)  357 us
    unnamed x2, blocking collectives  295 us
    dot_general x4, matrix products, head_backward(): jnp.einsum('qrk,qrd->kd', score_grad, query_one, preferred_element_type=j...  192 us
    dot_general x4, matrix products, head_backward(): jnp.einsum('qrk,kd->qrd', score_grad, key_one, preferred_element_type=jnp...  190 us
    unnamed x23, waiting for transfers between devices  167 us
  transfers between devices with their start and end apart: 25, of which 19 were waited for; matrix products, arithmetic and copies ran while one was open for 14% of the time, Pallas kernels for 0%

commit v1 on v0

v1 whole, which is shorter than its diff:
```python
import jax
import jax.numpy as jnp
from jax import lax
from jax.sharding import PartitionSpec as P

H = 24
KV = 8
HD = 64
TOPK = 8
PROMPT = 2048
CONT_LEN = 512


norm_eps = 1e-06
rope_base = 10000.0


def rotation(position):
    halfway = HD // 2
    freq = rope_base ** (-jnp.arange(halfway, dtype=jnp.float32) * 2.0 / HD)
    angle = position.astype(jnp.float32)[:, None] * freq[None, :]
    return (jnp.cos(angle)[:, None, :], jnp.sin(angle)[:, None, :])


def rotate(values, cosine, sine):
    halfway = HD // 2
    former = values[..., :halfway]
    latter = values[..., halfway:]
    return jnp.concatenate(
        [former * cosine - latter * sine, latter * cosine + former * sine], axis=-1
    )


def over_rows(left, right):
    return lax.dot_general(
        left, right, (((0,), (0,)), ((), ())), preferred_element_type=jnp.float32
    )


def over_cols(left, right):
    return lax.dot_general(
        left, right, (((1,), (1,)), ((), ())), preferred_element_type=jnp.float32
    )


def gather_spread(rows):
    part = rows.shape[0] // lax.axis_size("tp")
    mine = lax.dynamic_slice_in_dim(rows, lax.axis_index("tp") * part, part)
    return lax.all_gather(mine, ("ctx", "tp"), axis=0, tiled=True)


def sum_to_owner(terms):
    piece = lax.psum_scatter(
        terms.astype(jnp.bfloat16), ("ctx", "tp"), scatter_dimension=0, tiled=True
    )
    return lax.all_gather(piece, "tp", axis=0, tiled=True).astype(jnp.float32)


def on_device(
    tokens,
    routes,
    cotangent,
    attn_gain,
    moe_gain,
    w_query,
    w_key,
    w_value,
    w_out,
    w_router,
    w_gate,
    w_up,
    w_down,
):
    count, width = tokens.shape
    spread = lax.axis_size("ctx")
    place = lax.axis_index("ctx")
    tp_size = lax.axis_size("tp")
    group = count * spread
    query_cols, key_cols = w_query.shape[1], w_key.shape[1]
    qkv_full = lax.all_gather(
        jnp.concatenate([w_query, w_key, w_value], axis=1), "fsdp", axis=0, tiled=True
    )
    query_full = qkv_full[:, :query_cols]
    key_full = qkv_full[:, query_cols : query_cols + key_cols]
    value_full = qkv_full[:, query_cols + key_cols :]
    attn_scale = lax.all_gather(attn_gain, "fsdp", axis=0, tiled=True)
    moe_scale = lax.all_gather(moe_gain, "fsdp", axis=0, tiled=True)
    routes_all = lax.all_gather(routes, "ctx", axis=0)
    out_full = lax.all_gather(w_out, "fsdp", axis=1, tiled=True)
    router_full = lax.all_gather(w_router, "fsdp", axis=0, tiled=True)
    cotangent_all = gather_spread(cotangent).reshape(spread, count, width)
    hidden_units = w_gate.shape[2]
    joined = jnp.concatenate([w_gate, w_up, jnp.swapaxes(w_down, 1, 2)], axis=2)
    joined_full = lax.all_gather(joined, "fsdp", axis=1, tiled=True)
    gate_up_full = joined_full[:, :, : 2 * hidden_units]
    down_full = joined_full[:, :, 2 * hidden_units :]
    index_all = jnp.arange(group, dtype=jnp.int32)
    segment_all = jnp.where(index_all < PROMPT, 0, 1 + (index_all - PROMPT) // CONT_LEN)
    position_all = jnp.where(
        index_all < PROMPT, index_all, PROMPT + (index_all - PROMPT) % CONT_LEN
    )
    first_row = place * count
    row_index = lax.dynamic_slice_in_dim(index_all, first_row, count)
    row_segment = lax.dynamic_slice_in_dim(segment_all, first_row, count)
    row_position = lax.dynamic_slice_in_dim(position_all, first_row, count)
    allowed = (index_all[None, :] <= row_index[:, None]) & (
        (segment_all[None, :] == 0) | (segment_all[None, :] == row_segment[:, None])
    )
    cosine, sine = rotation(row_position)
    scale = HD ** (-0.5)
    ratio = H // KV
    kv_local = key_cols // HD

    experts = w_router.shape[1]
    capacity = max(tp_size, 9 * count * TOPK // (8 * experts) // tp_size * tp_size)
    padded = -(-capacity // 16) * 16
    local_experts = experts // spread
    first_expert = place * local_experts
    expert_ids = jnp.arange(experts, dtype=jnp.int32)
    local_ids = first_expert + jnp.arange(local_experts, dtype=jnp.int32)
    routes_t = jnp.swapaxes(routes_all, 1, 2)
    flags = jnp.any(routes_t[:, None, :, :] == local_ids[None, :, None, None], axis=2)
    earlier = jnp.arange(count)[:, None] < jnp.arange(count)[None, :]
    ranks = jnp.einsum(
        "beu,ut->bet",
        flags.astype(jnp.bfloat16),
        earlier.astype(jnp.bfloat16),
        preferred_element_type=jnp.float32,
    ).astype(jnp.int32)
    slot_of = jnp.where(flags & (ranks < capacity), ranks, -1)
    slot_ids = jnp.arange(padded, dtype=jnp.int32)
    chosen_slot = slot_of[:, :, None, :] == slot_ids[None, None, :, None]
    pick = chosen_slot.astype(jnp.bfloat16).reshape(spread, local_experts * padded, count)
    pick = lax.optimization_barrier(pick)

    def to_slots(rows):
        return jnp.einsum(
            "bjt,btd->bjd", pick, rows, preferred_element_type=jnp.float32
        ).astype(jnp.bfloat16).reshape(spread, local_experts, padded, width)

    def from_slots(slots):
        return jnp.einsum(
            "bjt,bjd->btd",
            pick,
            slots.reshape(spread, local_experts * padded, width),
            preferred_element_type=jnp.float32,
        ).reshape(group, width)

    cotangent_slots = to_slots(cotangent_all)

    token_f = tokens.astype(jnp.float32)
    inverse_one = lax.rsqrt(jnp.mean(token_f * token_f, axis=-1, keepdims=True) + norm_eps)
    unit_one = token_f * inverse_one
    normed_one = (unit_one * attn_scale.astype(jnp.float32)).astype(jnp.bfloat16)
    pre = jnp.dot(normed_one, qkv_full, preferred_element_type=jnp.float32)
    query_pre = pre[:, :query_cols].reshape(count, kv_local * ratio, HD)
    key_pre = pre[:, query_cols : query_cols + key_cols].reshape(count, kv_local, HD)
    query_b = (
        rotate(query_pre, cosine, sine).astype(jnp.bfloat16).reshape(count, kv_local, ratio, HD)
    )
    key_b = rotate(key_pre, cosine, sine).astype(jnp.bfloat16).reshape(count, kv_local * HD)
    value_b = pre[:, query_cols + key_cols :].astype(jnp.bfloat16)
    keys_values = lax.all_gather(
        jnp.concatenate([key_b, value_b], axis=1), "ctx", axis=0, tiled=True
    )
    query_heads = jnp.moveaxis(query_b, 1, 0)
    kv_heads = jnp.moveaxis(keys_values.reshape(group, 2 * kv_local, HD), 1, 0)
    key_heads, value_heads = kv_heads[:kv_local], kv_heads[kv_local:]

    def masked_scores(query_one, key_one):
        scores = (
            jnp.einsum("qrd,kd->qrk", query_one, key_one, preferred_element_type=jnp.float32)
            * scale
        )
        return jnp.where(allowed[:, None, :], scores, -1e30)

    def head_forward(operands):
        query_one, key_one, value_one = operands
        scores = masked_scores(query_one, key_one)
        highest = jnp.max(scores, axis=-1, keepdims=True)
        expo = jnp.exp(scores - highest)
        total = jnp.sum(expo, axis=-1, keepdims=True)
        probs = (expo / total).astype(jnp.bfloat16)
        mixed = jnp.einsum("qrk,kd->qrd", probs, value_one, preferred_element_type=jnp.float32)
        return (mixed, highest + jnp.log(total))

    head_out, log_sums = lax.map(head_forward, (query_heads, key_heads, value_heads))
    mixed_b = (
        jnp.moveaxis(head_out, 0, 1).reshape(count, kv_local * ratio * HD).astype(jnp.bfloat16)
    )
    attn_part = jnp.dot(mixed_b, out_full, preferred_element_type=jnp.float32)
    attn_total = lax.psum(attn_part, "tp")
    hidden = token_f + attn_total
    inverse_two = lax.rsqrt(jnp.mean(hidden * hidden, axis=-1, keepdims=True) + norm_eps)
    unit_two = hidden * inverse_two
    normed_two = (unit_two * moe_scale.astype(jnp.float32)).astype(jnp.bfloat16)
    normed_all = gather_spread(normed_two)
    logits = jnp.dot(normed_all, router_full, preferred_element_type=jnp.float32).reshape(
        spread, count, experts
    )
    hits = jnp.any(routes_all[:, :, :, None] == expert_ids, axis=2)
    highest_logit = jnp.max(jnp.where(hits, logits, -jnp.inf), axis=-1, keepdims=True)
    weight = jnp.where(hits, jnp.exp(jnp.where(hits, logits - highest_logit, 0.0)), 0.0)
    gates_all = weight / jnp.sum(weight, axis=-1, keepdims=True)
    gates = lax.dynamic_index_in_dim(gates_all, place, 0, keepdims=False)
    gates_local = jnp.swapaxes(
        lax.dynamic_slice_in_dim(gates_all, first_expert, local_experts, 2), 1, 2
    )
    slot_gate = jnp.sum(
        jnp.where(chosen_slot, gates_local[:, :, None, :], 0.0), axis=-1, keepdims=True
    )
    token_slots = to_slots(normed_all.reshape(spread, count, width))
    both_pre = jnp.einsum(
        "becd,edf->becf", token_slots, gate_up_full, preferred_element_type=jnp.float32
    )
    active_grad = jnp.einsum(
        "becd,edf->becf", cotangent_slots, down_full, preferred_element_type=jnp.float32
    )
    gate_pre, up_pre = both_pre[..., :hidden_units], both_pre[..., hidden_units:]
    sigma = jax.nn.sigmoid(gate_pre)
    silu_gate = gate_pre * sigma
    active = silu_gate * up_pre
    gate_grad_slots = jnp.sum(active * active_grad, axis=-1)
    active_weighted = (slot_gate * active).astype(jnp.bfloat16)
    weighted_grad = slot_gate * active_grad
    up_grad = weighted_grad * silu_gate
    gate_grad = weighted_grad * up_pre * sigma * (1.0 + gate_pre * (1.0 - sigma))
    both_grad = jnp.concatenate([gate_grad, up_grad], axis=-1).astype(jnp.bfloat16)
    active_weighted, both_grad = lax.optimization_barrier((active_weighted, both_grad))
    input_slots = jnp.einsum(
        "becf,edf->becd", both_grad, gate_up_full, preferred_element_type=jnp.float32
    ).astype(jnp.bfloat16)
    normed_grad = sum_to_owner(from_slots(input_slots))
    gate_grad_rows = jnp.swapaxes(
        jnp.sum(jnp.where(chosen_slot, gate_grad_slots[..., None], 0.0), axis=2), 1, 2
    )
    gate_grad_wide = lax.dynamic_update_slice_in_dim(
        jnp.zeros((spread, count, experts), jnp.float32), gate_grad_rows, first_expert, 2
    ).reshape(group, experts)
    gate_grad_own = lax.psum(
        lax.psum_scatter(gate_grad_wide, "ctx", scatter_dimension=0, tiled=True), "tp"
    )
    result_slots = jnp.einsum(
        "becf,edf->becd", active_weighted, down_full, preferred_element_type=jnp.float32
    ).astype(jnp.bfloat16)
    moe_sum = sum_to_owner(from_slots(result_slots))
    output = (hidden + moe_sum).astype(jnp.bfloat16)
    grad_gate_up = jnp.einsum(
        "becd,becf->edf", token_slots, both_grad, preferred_element_type=jnp.float32
    )
    grad_down = jnp.einsum(
        "becd,becf->edf", cotangent_slots, active_weighted, preferred_element_type=jnp.float32
    )
    joined_grad = lax.psum_scatter(
        jnp.concatenate([grad_gate_up, grad_down], axis=2).astype(jnp.bfloat16),
        "fsdp",
        scatter_dimension=1,
        tiled=True,
    ).astype(jnp.float32)

    grad_output = cotangent.astype(jnp.float32)
    logit_grad = (
        gates * (gate_grad_own - jnp.sum(gates * gate_grad_own, axis=-1, keepdims=True))
    ).astype(jnp.bfloat16)
    grad_router = over_rows(normed_two, logit_grad)
    normed_grad = normed_grad + over_cols(logit_grad, router_full)
    grad_moe_gain = jnp.sum(normed_grad * unit_two, axis=0)
    scaled_two = normed_grad * moe_scale.astype(jnp.float32)
    hidden_grad = grad_output + inverse_two * (
        scaled_two - unit_two * jnp.mean(scaled_two * unit_two, axis=-1, keepdims=True)
    )
    hidden_grad_b = hidden_grad.astype(jnp.bfloat16)
    grad_wout = over_rows(hidden_grad_b, mixed_b)
    lanes = 128
    thin = jnp.concatenate(
        [
            grad_router,
            grad_moe_gain[:, None],
            jnp.zeros((width, lanes - 1 - experts), jnp.float32),
        ],
        axis=1,
    )
    early = lax.psum_scatter(
        jnp.concatenate([grad_wout, thin], axis=1).astype(jnp.bfloat16),
        ("fsdp", "ctx"),
        scatter_dimension=0,
        tiled=True,
    ).astype(jnp.float32)
    out_rows = grad_wout.shape[1]
    mixed_grad = over_cols(hidden_grad_b, out_full).astype(jnp.bfloat16)
    mixed_heads = jnp.moveaxis(mixed_grad.reshape(count, kv_local, ratio, HD), 1, 0)

    def head_backward(operands):
        query_one, key_one, value_one, grad_one, log_sum = operands
        probs = jnp.exp(masked_scores(query_one, key_one) - log_sum)
        probs_b = probs.astype(jnp.bfloat16)
        prob_grad = jnp.einsum(
            "qrd,kd->qrk", grad_one, value_one, preferred_element_type=jnp.float32
        )
        value_grad = jnp.einsum(
            "qrk,qrd->kd", probs_b, grad_one, preferred_element_type=jnp.float32
        )
        delta = jnp.sum(probs * prob_grad, axis=-1, keepdims=True)
        score_grad = (probs * (prob_grad - delta) * scale).astype(jnp.bfloat16)
        query_grad = jnp.einsum(
            "qrk,kd->qrd", score_grad, key_one, preferred_element_type=jnp.float32
        )
        key_grad = jnp.einsum(
            "qrk,qrd->kd", score_grad, query_one, preferred_element_type=jnp.float32
        )
        return (query_grad, key_grad, value_grad)

    query_grads, key_grads, value_grads = lax.map(
        head_backward, (query_heads, key_heads, value_heads, mixed_heads, log_sums)
    )
    kv_terms = jnp.moveaxis(jnp.concatenate([key_grads, value_grads], axis=0), 0, 1).reshape(
        group, 2 * kv_local * HD
    )
    kv_sum = lax.psum_scatter(
        kv_terms.astype(jnp.bfloat16), "ctx", scatter_dimension=0, tiled=True
    ).astype(jnp.float32)
    key_sum, value_sum = kv_sum[:, :key_cols], kv_sum[:, key_cols:]
    key_grad_b = (
        rotate(key_sum.reshape(count, kv_local, HD), cosine, -sine)
        .reshape(count, kv_local * HD)
        .astype(jnp.bfloat16)
    )
    value_grad_b = value_sum.astype(jnp.bfloat16)
    query_grad_b = (
        rotate(jnp.moveaxis(query_grads, 0, 1).reshape(count, kv_local * ratio, HD), cosine, -sine)
        .reshape(count, kv_local * ratio * HD)
        .astype(jnp.bfloat16)
    )
    qkv_grad_b = jnp.concatenate([query_grad_b, key_grad_b, value_grad_b], axis=1)
    normed_one_part = over_cols(qkv_grad_b, qkv_full)
    normed_one_grad = lax.psum(normed_one_part.astype(jnp.bfloat16), "tp").astype(jnp.float32)
    grad_attn_gain = jnp.sum(normed_one_grad * unit_one, axis=0)
    grad_qkv = over_rows(normed_one, qkv_grad_b)
    late = lax.psum_scatter(
        jnp.concatenate([grad_qkv, jnp.broadcast_to(grad_attn_gain[:, None], (width, lanes))], axis=1).astype(jnp.bfloat16),
        ("fsdp", "ctx"),
        scatter_dimension=0,
        tiled=True,
    ).astype(jnp.float32)
    scaled_one = normed_one_grad * attn_scale.astype(jnp.float32)
    token_grad = hidden_grad + inverse_one * (
        scaled_one - unit_one * jnp.mean(scaled_one * unit_one, axis=-1, keepdims=True)
    )
    return (
        output,
        token_grad,
        late[:, query_cols + 2 * key_cols],
        early[:, out_rows + experts],
        late[:, :query_cols],
        late[:, query_cols : query_cols + key_cols],
        late[:, query_cols + key_cols : query_cols + 2 * key_cols],
        early[:, :out_rows].T,
        early[:, out_rows : out_rows + experts],
        joined_grad[:, :, :hidden_units],
        joined_grad[:, :, hidden_units : 2 * hidden_units],
        jnp.swapaxes(joined_grad[:, :, 2 * hidden_units :], 1, 2),
    )


def solution(mesh):
    return jax.shard_map(
        on_device,
        mesh=mesh,
        in_specs=(
            P(("fsdp", "ctx"), None),
            P(("fsdp", "ctx"), None),
            P(("fsdp", "ctx"), None),
            P("fsdp"),
            P("fsdp"),
            P("fsdp", "tp"),
            P("fsdp", "tp"),
            P("fsdp", "tp"),
            P("tp", "fsdp"),
            P("fsdp", None),
            P("ctx", "fsdp", "tp"),
            P("ctx", "fsdp", "tp"),
            P("ctx", "tp", "fsdp"),
        ),
        out_specs=(
            P(("fsdp", "ctx"), None),
            P(("fsdp", "ctx"), None),
            P(("fsdp", "ctx")),
            P(("fsdp", "ctx")),
            P(("fsdp", "ctx"), "tp"),
            P(("fsdp", "ctx"), "tp"),
            P(("fsdp", "ctx"), "tp"),
            P("tp", ("fsdp", "ctx")),
            P(("fsdp", "ctx"), None),
            P("ctx", "fsdp", "tp"),
            P("ctx", "fsdp", "tp"),
            P("ctx", "tp", "fsdp"),
        ),
        check_vma=False,
    )
```

time: 4620 us -> 2310 us (0.50)
  waiting for transfers between devices: 2560 us -> 929 us
  local copies, waits for them, and re-layouts: 543 us -> 205 us
  blocking collectives: 344 us -> 42.4 us
  other arithmetic: 244 us -> 187 us
  matrix products: 867 us -> 922 us
    all_to_all x4 -> x0, waiting for transfers between devices: 1530 us -> none  [the longest x1 399 us: on_device(): lax.all_to_all(input_sel, 'ctx', split_axis=0, concat_axis=0, tiled=True)]
    reduce_scatter x8 -> x4, waiting for transfers between devices: 615 us -> 200 us  [the longest x2 139 us: sum_to_owner(): lax.psum_scatter(terms.astype(jnp.bfloat16), ('ctx', 'tp'), scatter_dimen...]
    unnamed x2 -> x0, blocking collectives: 295 us -> none
    gather x7 -> x0, local copies, waits for them, and re-layouts: 255 us -> none  [the longest x2 78.2 us: on_device(): grad_output[owners]]
    unnamed x23 -> x21, waiting for transfers between devices: 167 us -> 322 us
    all_gather x9 -> x8, waiting for transfers between devices: 229 us -> 372 us  [the longest x1 178 us: on_device(): joined_full = lax.all_gather(joined, 'fsdp', axis=1, tiled=True)]
    unnamed x144 -> x109, local copies, waits for them, and re-layouts: 51.2 us -> 135 us
    dot_general x13, matrix products: 178 us -> 239 us  [the longest x2 55.6 us: from_slots(): jnp.einsum('bjt,bjd->btd', pick, slots.reshape(spread, local_experts * pa...]
  transfers between devices with their start and end apart: 25 -> 18, of which waited for: 19 -> 15; matrix products, arithmetic and copies ran while one was open for 14% -> 24% of each run, Pallas kernels for 0% -> 0%
where the time goes in v1:
time: 2310 us; the launch traced here: 2300 us
  waiting for transfers between devices  929 us (40%)
  matrix products  922 us (40%)
  local copies, waits for them, and re-layouts  205 us (9%)
  other arithmetic  187 us (8%)
  blocking collectives  42.4 us (2%)
    unnamed x21, waiting for transfers between devices  322 us
    dot_general x4, matrix products, head_backward(): jnp.einsum('qrk,qrd->kd', score_grad, query_one, preferred_element_type=j...  193 us
    dot_general x4, matrix products, head_backward(): jnp.einsum('qrk,kd->qrd', score_grad, key_one, preferred_element_type=jnp...  191 us
    all_gather x1, waiting for transfers between devices, on_device(): joined_full = lax.all_gather(joined, 'fsdp', axis=1, tiled=True)  178 us
    reduce_scatter x2, waiting for transfers between devices, sum_to_owner(): lax.psum_scatter(terms.astype(jnp.bfloat16), ('ctx', 'tp'), scatter_dimen...  139 us
    unnamed x109, local copies, waits for them, and re-layouts  135 us
    dot_general x8, matrix products, masked_scores(): jnp.einsum('qrd,kd->qrk', query_one, key_one, preferred_element_type=jnp....  101 us
    all_gather x2, waiting for transfers between devices, gather_spread(): return lax.all_gather(mine, ('ctx', 'tp'), axis=0, tiled=True)  81 us
  transfers between devices with their start and end apart: 18, of which 15 were waited for; matrix products, arithmetic and copies ran while one was open for 24% of the time, Pallas kernels for 0%

profile of v1, /device:TPU:0, one launch (start us, length us, event | category | flops | bytes accessed | tf_op | source)
XLA Modules:
  0.0 2305.0 jit_solution(5933719670001664309)
XLA Ops:
  24.6 39.8 %all-gather.12.cloned.1.call-done = bf16[1536,1280]{1,0:T(8,128)(2,1)} async-done(((bf16[384,1280]{1,0:T(8,128)(2,1)}), bf16[1536,1280]{1,0:T(8,128)(2,1)}) %all-gather.12.cloned.1.call-update) | async-done | bytes 3932176 | tf_op jit(solution)/shard_map/all_gather | solution.py:80
  82.4 54.5 %all-gather.14.cloned.1.call-done = bf16[3072,512]{1,0:T(8,128)(2,1)} async-done(((bf16[768,512]{1,0:T(8,128)(2,1)}), bf16[3072,512]{1,0:T(8,128)(2,1)}) %all-gather.14.cloned.1.call-update) | async-done | bytes 3145744 | tf_op jit(solution)/shard_map/all_gather | solution.py:163
  142.1 176.4 %while.30 = (s32[]{:T(128)}, bf16[4,768,3,64]{1,3,2,0:T(8,128)(2,1)}, f32[4,768,3,1]{1,2,3,0:T(4,128)}, bf16[4,768,3,64]{1,3,2,0:T(8,128)(2,1)}, bf16[4,3072,64]...) while((s32[]{:T(128)}, ...), condition=%wide.region_4.5_spmd.clone.clone, body=%wide.region_1.4_spmd.clone.sunk.clone | while | flops 1906308864 | bytes 105587360 | solution.py:187
  145.5 13.1 fusion.234
  158.6 13.1 fusion.235
  335.8 16.6 all-reduce.4.cloned.1.call-done
  369.4 15.8 all-gather
  402.9 15.3 all-gather.22.cloned.1.call-done
  418.1 25.4 %convolution_convert_fusion = bf16[4,1760,1536]{2,1,0:T(8,128)(2,1)} fusion(bf16[4,1760,768]{2,1,0:T(8,128)(2,1)} %fusion.107, bf16[4,768,1536]{2,1,0:T(8,128)(2,1)} %bitcast.287), kind=kOutput, calls=%fused_computation.81 | convolution fusion | flops 16620257280 | bytes 41877504 | tf_op jit(solution)/shard_map/bjt,btd->bjd/dot_general | solution.py:137
  443.5 65.8 %all-gather.20.cloned.1.call-done = bf16[3072,1536]{1,0:T(8,128)(2,1)} async-done(((bf16[384,1536]{1,0:T(8,128)(2,1)}), bf16[3072,1536]{1,0:T(8,128)(2,1)}) %all-gather.20.cloned.1.call-update) | async-done | bytes 9437200 | tf_op jit(solution)/shard_map/all_gather | solution.py:49
  517.0 28.5 %convolution_convert_fusion.1 = bf16[4,1760,1536]{2,1,0:T(8,128)(2,1)} fusion(bf16[4,1760,768]{2,1,0:T(8,128)(2,1)} %fusion.107, bf16[4,768,1536]{2,1,0:T(8,128)(2,1)} %bitcast.259), kind=kOutput, calls=%fused_computation.82 | convolution fusion | flops 16620257280 | bytes 41877504 | tf_op jit(solution)/shard_map/bjt,btd->bjd/dot_general | solution.py:137
  545.5 178.5 %all-gather.18.cloned.1.call-done = bf16[10,1536,768]{2,1,0:T(8,128)(2,1)} async-done(((bf16[10,384,768]{2,1,0:T(8,128)(2,1)}), bf16[10,1536,768]{2,1,0:T(8,128)(2,1)}) %all-gather.18.cloned.1.call-update) | async-done | bytes 23592976 | tf_op jit(solution)/shard_map/all_gather | solution.py:94
  723.9 23.4 %fusion.108 = f32[4,10,176,512]{3,2,0,1:T(8,128)} fusion(bf16[4,10,176,1536]{3,2,1,0:T(8,128)(2,1)} %bitcast.290, bf16[10,1536,768]{2,1,0:T(8,128)(2,1)} %all-gather.18.cloned.1.call-done), kind=kOutput, calls=%fused_computation.97 | convolution fusion | flops 11072962560 | bytes 51773440 | tf_op jit(solution)/shard_map/becd,edf->becf/dot_general | solution.py:213
  747.3 18.6 fusion.111
  790.5 21.2 convert_bitcast_fusion
  811.6 17.5 copy.118
  830.6 27.8 %convolution_convert_fusion.3 = bf16[4,768,1536]{2,1,0:T(8,128)(2,1)} fusion(bf16[4,1760,768]{2,1,0:T(8,128)(2,1)} %fusion.107, bf16[4,1760,1536]{2,1,0:T(8,128)(2,1)} %bitcast.257), kind=kOutput, calls=%fused_computation.117 | convolution fusion | flops 16614162432 | bytes 41877504 | tf_op jit(solution)/shard_map/bjt,bjd->btd/dot_general | solution.py:142
  858.5 14.3 convert_bitcast_fusion.1
  872.8 17.7 copy.117
  890.5 27.9 %convolution_convert_fusion.4 = bf16[4,768,1536]{2,1,0:T(8,128)(2,1)} fusion(bf16[4,1760,768]{2,1,0:T(8,128)(2,1)} %fusion.107, bf16[4,1760,1536]{2,1,0:T(8,128)(2,1)} %bitcast.258), kind=kOutput, calls=%fused_computation.118 | convolution fusion | flops 16614162432 | bytes 41877504 | tf_op jit(solution)/shard_map/bjt,bjd->btd/dot_general | solution.py:142
  919.2 38.6 %reduce-scatter.16.cloned.1.call-done = bf16[384,1536]{1,0:T(8,128)(2,1)} async-done(((bf16[3072,1536]{1,0:T(8,128)(2,1)}), bf16[384,1536]{1,0:T(8,128)(2,1)}) %reduce-scatter.16.cloned.1.call-update) | async-done | bytes 1179664 | tf_op jit(solution)/shard_map/reduce_scatter | solution.py:53
  957.9 100.2 %reduce-scatter.14.cloned.1.call-done = bf16[384,1536]{1,0:T(8,128)(2,1)} async-done(((bf16[3072,1536]{1,0:T(8,128)(2,1)}), bf16[384,1536]{1,0:T(8,128)(2,1)}) %reduce-scatter.14.cloned.1.call-update) | async-done | bytes 1179664 | tf_op jit(solution)/shard_map/reduce_scatter | solution.py:53
  1058.2 18.6 all-reduce.6.cloned.1.call-done
  1113.6 565.2 %while.31 = (s32[]{:T(128)}, f32[4,768,3,64]{1,3,2,0:T(8,128)}, bf16[4,3072,64]{1,2,0:T(8,128)(2,1)}, bf16[4,3072,64]{1,2,0:T(8,128)(2,1)}, bf16[4,768,3,64]{1,3...) while((s32[]{:T(128)}, f32[4,768,3,64]{1,3,2,0:T(8,128)}, ...), condition=%wide.region_22.23_spmd.clone.clone, body=%wide.region_20.22_spmd.clone.sunk.clone | while | flops 4723321344 | bytes 330236064 | solution.py:313
  1126.1 14.3 fusion.247
  1145.1 47.7 %fusion.250 = f32[4,768,3,64]{1,3,2,0:T(8,128)} fusion(f32[4,768,3,64]{1,3,2,0:T(8,128)} %get-tuple-element.558, s32[]{:T(128)} %get-tuple-element.557, f32[768,3,3072]{2,0,1:T(8,128)} %fusion.247, f32[768,3,3072]{2,0,1:T(8,128)} %fusion.248, f32[768,3]{0,1:T(4,128)} %dynamic-slice_bitcast_fusion.4, pred[768,3072]{1,0:T(8,128)(4,1)S(1)} %fusion.249, ...), kind=kOutput, calls=%fused_computation.49.clone.1.clone | convolution fusion | flops 983831808 | bytes 118973440 | tf_op jit(solution)/shard_map/while/body/eval_jaxpr/qrk,kd->qrd/dot_general | solution.py:305
  1192.8 48.3 %fusion.251 = bf16[4,3072,64]{1,2,0:T(8,128)(2,1)} fusion(bf16[4,3072,64]{1,2,0:T(8,128)(2,1)} %get-tuple-element.559, s32[]{:T(128)} %get-tuple-element.557, f32[768,3,3072]{2,0,1:T(8,128)} %fusion.247, f32[768,3,3072]{2,0,1:T(8,128)} %fusion.248, f32[768,3]{0,1:T(4,128)} %dynamic-slice_bitcast_fusion.4, pred[768,3072]{1,0:T(8,128)(4,1)S(1)} %fusion.249, ...), kind=kOutput, calls=%fused_computation.47.clone.1.clone | convolution fusion | flops 983831808 | bytes 119071744 | tf_op jit(solution)/shard_map/while/body/eval_jaxpr/qrk,qrd->kd/dot_general | solution.py:308
  1241.1 13.9 fusion.252
  1267.2 14.3 fusion.247
  1286.2 47.7 %fusion.250 = f32[4,768,3,64]{1,3,2,0:T(8,128)} fusion(f32[4,768,3,64]{1,3,2,0:T(8,128)} %get-tuple-element.558, s32[]{:T(128)} %get-tuple-element.557, f32[768,3,3072]{2,0,1:T(8,128)} %fusion.247, f32[768,3,3072]{2,0,1:T(8,128)} %fusion.248, f32[768,3]{0,1:T(4,128)} %dynamic-slice_bitcast_fusion.4, pred[768,3072]{1,0:T(8,128)(4,1)S(1)} %fusion.249, ...), kind=kOutput, calls=%fused_computation.49.clone.1.clone | convolution fusion | flops 983831808 | bytes 118973440 | tf_op jit(solution)/shard_map/while/body/eval_jaxpr/qrk,kd->qrd/dot_general | solution.py:305
  1333.9 48.3 %fusion.251 = bf16[4,3072,64]{1,2,0:T(8,128)(2,1)} fusion(bf16[4,3072,64]{1,2,0:T(8,128)(2,1)} %get-tuple-element.559, s32[]{:T(128)} %get-tuple-element.557, f32[768,3,3072]{2,0,1:T(8,128)} %fusion.247, f32[768,3,3072]{2,0,1:T(8,128)} %fusion.248, f32[768,3]{0,1:T(4,128)} %dynamic-slice_bitcast_fusion.4, pred[768,3072]{1,0:T(8,128)(4,1)S(1)} %fusion.249, ...), kind=kOutput, calls=%fused_computation.47.clone.1.clone | convolution fusion | flops 983831808 | bytes 119071744 | tf_op jit(solution)/shard_map/while/body/eval_jaxpr/qrk,qrd->kd/dot_general | solution.py:308
  1382.2 13.9 fusion.252
  1408.4 14.3 fusion.247
  1427.4 47.7 %fusion.250 = f32[4,768,3,64]{1,3,2,0:T(8,128)} fusion(f32[4,768,3,64]{1,3,2,0:T(8,128)} %get-tuple-element.558, s32[]{:T(128)} %get-tuple-element.557, f32[768,3,3072]{2,0,1:T(8,128)} %fusion.247, f32[768,3,3072]{2,0,1:T(8,128)} %fusion.248, f32[768,3]{0,1:T(4,128)} %dynamic-slice_bitcast_fusion.4, pred[768,3072]{1,0:T(8,128)(4,1)S(1)} %fusion.249, ...), kind=kOutput, calls=%fused_computation.49.clone.1.clone | convolution fusion | flops 983831808 | bytes 118973440 | tf_op jit(solution)/shard_map/while/body/eval_jaxpr/qrk,kd->qrd/dot_general | solution.py:305
  1475.1 48.3 %fusion.251 = bf16[4,3072,64]{1,2,0:T(8,128)(2,1)} fusion(bf16[4,3072,64]{1,2,0:T(8,128)(2,1)} %get-tuple-element.559, s32[]{:T(128)} %get-tuple-element.557, f32[768,3,3072]{2,0,1:T(8,128)} %fusion.247, f32[768,3,3072]{2,0,1:T(8,128)} %fusion.248, f32[768,3]{0,1:T(4,128)} %dynamic-slice_bitcast_fusion.4, pred[768,3072]{1,0:T(8,128)(4,1)S(1)} %fusion.249, ...), kind=kOutput, calls=%fused_computation.47.clone.1.clone | convolution fusion | flops 983831808 | bytes 119071744 | tf_op jit(solution)/shard_map/while/body/eval_jaxpr/qrk,qrd->kd/dot_general | solution.py:308
  1523.4 13.9 fusion.252
  1549.5 14.3 fusion.247
  1568.5 47.7 %fusion.250 = f32[4,768,3,64]{1,3,2,0:T(8,128)} fusion(f32[4,768,3,64]{1,3,2,0:T(8,128)} %get-tuple-element.558, s32[]{:T(128)} %get-tuple-element.557, f32[768,3,3072]{2,0,1:T(8,128)} %fusion.247, f32[768,3,3072]{2,0,1:T(8,128)} %fusion.248, f32[768,3]{0,1:T(4,128)} %dynamic-slice_bitcast_fusion.4, pred[768,3072]{1,0:T(8,128)(4,1)S(1)} %fusion.249, ...), kind=kOutput, calls=%fused_computation.49.clone.1.clone | convolution fusion | flops 983831808 | bytes 118973440 | tf_op jit(solution)/shard_map/while/body/eval_jaxpr/qrk,kd->qrd/dot_general | solution.py:305
  1616.2 48.3 %fusion.251 = bf16[4,3072,64]{1,2,0:T(8,128)(2,1)} fusion(bf16[4,3072,64]{1,2,0:T(8,128)(2,1)} %get-tuple-element.559, s32[]{:T(128)} %get-tuple-element.557, f32[768,3,3072]{2,0,1:T(8,128)} %fusion.247, f32[768,3,3072]{2,0,1:T(8,128)} %fusion.248, f32[768,3]{0,1:T(4,128)} %dynamic-slice_bitcast_fusion.4, pred[768,3072]{1,0:T(8,128)(4,1)S(1)} %fusion.249, ...), kind=kOutput, calls=%fused_computation.47.clone.1.clone | convolution fusion | flops 983831808 | bytes 119071744 | tf_op jit(solution)/shard_map/while/body/eval_jaxpr/qrk,qrd->kd/dot_general | solution.py:308
  1664.5 13.9 fusion.252
  1683.4 61.2 %reduce-scatter.20.cloned.1.call-done = bf16[768,512]{0,1:T(8,128)(2,1)} async-done(((bf16[3072,512]{0,1:T(8,128)(2,1)}), bf16[768,512]{0,1:T(8,128)(2,1)}) %reduce-scatter.20.cloned.1.call-update) | async-done | bytes 786448 | tf_op jit(solution)/shard_map/reduce_scatter | solution.py:319
  1786.8 15.4 bitcast_convert_fusion.1
  1802.2 24.1 %bitcast_convert_fusion = bf16[10,1536,512]{1,2,0:T(8,128)(2,1)} fusion(bf16[4,10,176,1536]{3,2,1,0:T(8,128)(2,1)} %bitcast.291, bf16[4,10,176,512]{3,2,0,1:T(8,128)(2,1)} %pad_maximum_fusion.1), kind=kOutput, calls=%fused_computation.80 | convolution fusion | flops 11080826880 | bytes 44564480 | tf_op jit(solution)/shard_map/becd,becf->edf/dot_general | solution.py:248
  1826.3 19.8 pad_maximum_fusion
  1846.1 44.9 %copy.135 = bf16[10,1536,768]{2,0,1:T(8,128)(2,1)} copy(bf16[10,1536,768]{1,2,0:T(8,128)(2,1)} %pad_maximum_fusion) | data formatting | bytes 47185920
  1891.1 27.0 %copy.140 = bf16[192,8,10,768]{3,1,2,0:T(8,128)(2,1)} copy(bf16[192,8,10,768]{3,2,1,0:T(8,128)(2,1)} %bitcast.254) | data formatting | bytes 47185920
  1927.9 113.4 %reduce-scatter.22.cloned.1.call-done = bf16[96,1408]{1,0:T(8,128)(2,1)} async-done(((bf16[1536,1408]{1,0:T(8,128)(2,1)}), bf16[96,1408]{1,0:T(8,128)(2,1)}) %reduce-scatter.22.cloned.1.call-update) | async-done | bytes 270352
  2045.4 206.8 %reduce-scatter.26.cloned.1.call-done = bf16[384,7680]{1,0:T(8,128)(2,1)} async-done(((bf16[1536,7680]{1,0:T(8,128)(2,1)}), bf16[384,7680]{1,0:T(8,128)(2,1)}) %reduce-scatter.26.cloned.1.call-update) | async-done | bytes 5898256
  (315 shorter events, 485.9 us)
Async XLA Ops:
  8.0 56.4 %copy-start.2 = (bf16[768,1536]{1,0:T(8,128)(2,1)S(1)}, bf16[768,1536]{1,0:T(8,128)(2,1)}, u32[]{:S(2)}) copy-start(bf16[768,1536]{1,0:T(8,128)(2,1)} %param.17) | copy-start | bytes 7077892
  8.0 56.4 %all-gather.12.cloned.1.call-start = ((), (), s32[]{:S(2)}) async-start(), calls=%async_computation.7 | async-start | bytes 4915200 | tf_op jit(solution)/shard_map/all_gather | solution.py:80
  10.5 126.4 %all-gather.14.cloned.1.call-start = ((), (), s32[]{:S(2)}) async-start(), calls=%async_computation.8 | async-start | bytes 3932160 | tf_op jit(solution)/shard_map/all_gather | solution.py:163
  20.9 48.9 %copy-start.39 = (f32[1536]{0:T(1024)}, f32[1536]{0:T(1024)S(1)}, u32[]{:S(2)}) copy-start(f32[1536]{0:T(1024)S(1)} %reshape.290) | copy-start | bytes 18436
  23.5 46.3 %copy-start.43 = (f32[768]{0:T(1024)}, f32[768]{0:T(1024)S(1)}, u32[]{:S(2)}) copy-start(f32[768]{0:T(1024)S(1)} %add_rsqrt_fusion.1) | copy-start | bytes 9220
  24.6 56.5 %copy-start.15 = (f32[768,32]{0,1:T(8,128)}, f32[768,32]{0,1:T(8,128)S(1)}, u32[]{:S(2)}) copy-start(f32[768,32]{0,1:T(8,128)S(1)} %get-tuple-element.310) | copy-start | bytes 294916
  73.3 245.2 %all-gather.16.cloned.1.call-start = ((), (), s32[]{:S(2)}) async-start(), calls=%async_computation.9 | async-start | bytes 2949120 | tf_op jit(solution)/shard_map/all_gather | solution.py:89
  74.1 278.3 %all-reduce.4.cloned.1.call-start = ((), (), s32[]{:S(2)}) async-start(), calls=%async_computation.10 | async-start | bytes 9437184 | tf_op jit(solution)/shard_map/psum | solution.py:192
  158.5 13.8 copy-start.10
  202.9 13.5 copy-start.10
  246.9 13.5 copy-start.10
  290.9 13.5 copy-start.10
  318.5 6.3 copy-start.31
  318.5 6.3 copy-start.35
  324.8 27.6 %copy-start.3 = (bf16[768,1536]{1,0:T(8,128)(2,1)S(1)}, bf16[768,1536]{1,0:T(8,128)(2,1)}, u32[]{:S(2)}) copy-start(bf16[768,1536]{1,0:T(8,128)(2,1)} %param.17) | copy-start | bytes 7077892
  324.8 93.3 %all-gather.22.cloned.1.call-start = ((), (), s32[]{:S(2)}) async-start(), calls=%async_computation.13 | async-start | bytes 10616832 | tf_op jit(solution)/shard_map/all_gather | solution.py:49
  327.4 181.8 %all-gather.20.cloned.1.call-start = ((), (), s32[]{:S(2)}) async-start(), calls=%async_computation.12 | async-start | bytes 10616832 | tf_op jit(solution)/shard_map/all_gather | solution.py:49
  335.8 19.7 copy-start.37
  360.6 363.3 %all-gather.18.cloned.1.call-start = ((), (), s32[]{:S(2)}) async-start(), calls=%async_computation.11 | async-start | bytes 29491200 | tf_op jit(solution)/shard_map/all_gather | solution.py:94
  368.7 549.8 %reduce-scatter.18.cloned.1.call-start = ((), (), s32[]{:S(2)}) async-start(), calls=%async_computation.18 | async-start | bytes 614400 | tf_op jit(solution)/shard_map/reduce_scatter | solution.py:241
  386.7 7.2 copy-start.45
  402.9 106.4 %copy-start.25 = (bf16[1536,40]{0,1:T(8,128)(2,1)}, bf16[1536,40]{0,1:T(8,128)(2,1)S(1)}, u32[]{:S(2)}) copy-start(bf16[1536,40]{0,1:T(8,128)(2,1)S(1)} %all_gather.48) | copy-start | bytes 368644
  830.6 127.3 %reduce-scatter.16.cloned.1.call-start = ((), (), s32[]{:S(2)}) async-start(), calls=%async_computation.16 | async-start | bytes 10616832 | tf_op jit(solution)/shard_map/reduce_scatter | solution.py:53
  858.4 199.7 %reduce-scatter.14.cloned.1.call-start = ((), (), s32[]{:S(2)}) async-start(), calls=%async_computation.14 | async-start | bytes 10616832 | tf_op jit(solution)/shard_map/reduce_scatter | solution.py:53
  918.4 158.4 %copy-start.20 = (f32[4,768,40]{1,2,0:T(8,128)S(1)}, f32[4,768,40]{1,2,0:T(8,128)}, u32[]{:S(2)}) copy-start(f32[4,768,40]{1,2,0:T(8,128)} %copy-done.19) | copy-start | bytes 1474564
  918.4 172.2 %copy-start.26 = (bf16[1536,40]{0,1:T(8,128)(2,1)S(1)}, bf16[1536,40]{0,1:T(8,128)(2,1)}, u32[]{:S(2)}) copy-start(bf16[1536,40]{0,1:T(8,128)(2,1)} %copy-done.25) | copy-start | bytes 368644
  918.4 172.2 %copy-start.38 = (f32[1536]{0:T(1024)S(1)}, f32[1536]{0:T(1024)}, u32[]{:S(2)}) copy-start(f32[1536]{0:T(1024)} %copy-done.37) | copy-start | bytes 18436
  918.4 172.2 %copy-start.42 = (f32[768]{0:T(1024)S(1)}, f32[768]{0:T(1024)}, u32[]{:S(2)}) copy-start(f32[768]{0:T(1024)} %copy-done.41) | copy-start | bytes 9220
  918.4 158.3 %all-reduce.6.cloned.1.call-start = ((), (), s32[]{:S(2)}) async-start(), calls=%async_computation.19 | async-start | bytes 245760 | tf_op jit(solution)/shard_map/psum | solution.py:240
  919.2 171.4 %all-gather.26.cloned.1.call-start = ((), (), s32[]{:S(2)}) async-start(), calls=%async_computation.17 | async-start | bytes 3538944 | tf_op jit(solution)/shard_map/all_gather | solution.py:56
  957.9 146.2 %all-gather.24.cloned.1.call-start = ((), (), s32[]{:S(2)}) async-start(), calls=%async_computation.15 | async-start | bytes 3538944 | tf_op jit(solution)/shard_map/all_gather | solution.py:56
  1058.1 686.5 %reduce-scatter.20.cloned.1.call-start = ((), (), s32[]{:S(2)}) async-start(), calls=%async_computation.20 | async-start | bytes 3932160 | tf_op jit(solution)/shard_map/reduce_scatter | solution.py:319
  1078.6 19.3 copy-start.28
  1078.6 25.5 %copy-start.9 = (bf16[768,1536]{1,0:T(8,128)(2,1)S(1)}, bf16[768,1536]{1,0:T(8,128)(2,1)}, u32[]{:S(2)}) copy-start(bf16[768,1536]{1,0:T(8,128)(2,1)} %param.19) | copy-start | bytes 7077892
  1104.1 6.4 copy-start.18
  1126.1 15.6 copy-start.32
  1126.1 15.6 copy-start.36
  1267.2 15.6 copy-start.32
  1267.2 15.6 copy-start.36
  1408.4 15.6 copy-start.32
  1408.4 15.6 copy-start.36
  1549.5 15.6 copy-start.32
  1549.5 15.6 copy-start.36
  1682.9 91.5 %all-reduce.8.cloned.1.call-start = ((), (), s32[]{:S(2)}) async-start(), calls=%async_computation.21 | async-start | bytes 4718592 | tf_op jit(solution)/shard_map/psum | solution.py:336
  1683.4 63.9 %copy-start.23 = (bf16[768,12,64]{0,2,1:T(8,128)(2,1)}, bf16[768,12,64]{0,2,1:T(8,128)(2,1)S(1)}, u32[]{:S(2)}) copy-start(bf16[768,12,64]{0,2,1:T(8,128)(2,1)S(1)} %pad_maximum_fusion.6) | copy-start | bytes 3538948
  1752.5 165.5 %reduce-scatter.24.cloned.1.call-start = ((), (), s32[]{:S(2)}) async-start(), calls=%async_computation.23 | async-start | bytes 2924544
  1767.8 273.4 %reduce-scatter.22.cloned.1.call-start = ((), (), s32[]{:S(2)}) async-start(), calls=%async_computation.22 | async-start | bytes 4595712
  1786.7 465.5 %reduce-scatter.26.cloned.1.call-start = ((), (), s32[]{:S(2)}) async-start(), calls=%async_computation.24 | async-start | bytes 29491200
  (32 other events, 94.3 us)
Sparse Core Ops, SparseCore 0:
  11.3 53.1 all-gather.11
  73.4 63.4 all-gather.13
  138.7 35.8 all-gather.15
  324.9 27.3 all-reduce.3
  830.7 21.3 reduce-scatter.17
  858.5 99.2 reduce-scatter.15
  960.2 97.8 reduce-scatter.13
  1060.4 16.3 all-reduce.5
  1078.3 12.2 all-gather.25
  1092.0 12.1 all-gather.23
  1683.0 61.5 reduce-scatter.19
  1752.7 21.6 all-reduce.7
Sparse Core Ops, SparseCore 1:
  327.5 90.5 all-gather.21
  420.2 89.0 all-gather.19
  511.0 212.9 all-gather.17
  1767.9 130.7 reduce-scatter.23
  1903.8 137.4 reduce-scatter.21
  2044.4 207.8 reduce-scatter.25
